TPU v7x, 32 devices: a whole 2x2x4 slice. The times are simulated.
32 devices in a mesh: leaf: 8 (over z, y), front: 4 (over x, core).
Axes of the slice: x: 2, y: 2, z: 4, core: 2. Of those that a mesh axis runs over, the one named last changes fastest.
Arguments:
- right_side: float32 [8, 4, 96, 512], P('leaf', 'front'), may hold values from -6 to 6
- factor_inverse: float32 [8, 4, 128, 7680], P('leaf', 'front'), may hold values from -1 to 1, as said below
- update_panel: float32 [8, 4, 128, 1792], P('leaf', 'front'), may hold values from -0.09375 to 0.09375
- update_targets: int32 [8, 14], P('leaf'), may hold values from 0 to 31, as said below
- pivot_pairs: int32 [8, 4, 256], P('leaf', 'front'), may hold values 0 or 1
- pivot_diagonal: float32 [8, 4, 512], P('leaf', 'front'), may hold values from 0.5 to 2
- pivot_coupling: float32 [8, 4, 256], P('leaf', 'front'), may hold values from 3 to 5
Outputs:
- solution: float32 [8, 4, 96, 512], P('leaf', 'front')
Inputs may be any that keep to these rules, and one draw needn't show every extreme that they name: `factor_inverse`: each front's inverse factor is lower triangular in the front's row order with ones on its diagonal. `update_targets`: each front's list names distinct blocks of its parent's pivot rows in rising order, and is repeated in the row of every leaf index of the front's group.
All inputs are finite; a program needn't handle non-finite values. No bound on the sum of `pivot_pairs` on one device may be relied on, other than what follows from the above.
Results may differ from a plain program's by a relative error of at most 0.0001.
Values sent between devices are 32-bit elements; how exact they have to be, the bound alone decides.
A program may use at most 64 MiB of HBM per device.

v0:
```python
import jax
import jax.numpy as jnp
from jax import lax
from jax.sharding import PartitionSpec as P

LEVELS = 4
BLOCK = 128


exact_mode = lax.Precision.HIGHEST


def from_partner(block, axis, bit):
    count = lax.axis_size(axis)
    route = []
    for low in range(count):
        high = low | 1 << bit
        if high != low and high < count:
            route += [(low, high), (high, low)]
    return lax.ppermute(block, axis, route)


def pair_gather(values, bit_count, leaf_index):
    for bit_index in range(bit_count):
        partner = from_partner(values, "leaf", bit_index)
        is_upper = leaf_index >> bit_index & 1 == 1
        values = jnp.where(
            is_upper, jnp.concatenate([partner, values], 1), jnp.concatenate([values, partner], 1)
        )
    return values


def group_gather(values, bit_count, leaf_index):
    joined = pair_gather(values, bit_count, leaf_index)
    return lax.all_gather(joined, "front", axis=1, tiled=True)


def group_scatter(partial_terms, bit_count, leaf_index):
    share_sum = lax.psum_scatter(partial_terms, "front", scatter_dimension=1, tiled=True)
    for bit_index in reversed(range(bit_count)):
        half_width = share_sum.shape[1] // 2
        lower_half = share_sum[:, :half_width]
        higher = share_sum[:, half_width:]
        is_upper = leaf_index >> bit_index & 1 == 1
        kept_half = jnp.where(is_upper, higher, lower_half)
        sent_half = jnp.where(is_upper, lower_half, higher)
        share_sum = kept_half + from_partner(sent_half, "leaf", bit_index)
    return share_sum


def block_table(target_list, parent_blocks):
    ids = jnp.arange(parent_blocks, dtype=jnp.int32)
    return (target_list[:, None] == ids[None, :]).astype(jnp.float32)


def pivot_solve(solved, pivot_diag, couple, pivot_kinds):
    side_count = solved.shape[0]
    paired = solved.reshape(side_count, -1, 2)
    pair_first = paired[:, :, 0]
    second = paired[:, :, 1]
    diag_first = pivot_diag[0::2][None, :]
    diag_second = pivot_diag[1::2][None, :]
    coupling = couple[None, :]
    pair_flag = (pivot_kinds == 1)[None, :]
    determinant = diag_first * diag_second - coupling * coupling
    two_first = (diag_second * pair_first - coupling * second) / determinant
    two_second = (diag_first * second - coupling * pair_first) / determinant
    result_first = jnp.where(pair_flag, two_first, pair_first / diag_first)
    result_second = jnp.where(pair_flag, two_second, second / diag_second)
    return jnp.stack([result_first, result_second], axis=2).reshape(solved.shape)


def per_device(
    right_side,
    factor_inverse,
    update_panel,
    update_targets,
    pivot_pairs,
    pivot_diagonal,
    pivot_coupling,
):
    right_sides = right_side[0, 0]
    inverse = factor_inverse[0, 0]
    update_rows = update_panel[0, 0]
    targets = update_targets[0]
    pivot_kinds = pivot_pairs[0, 0]
    pivot_diag = pivot_diagonal[0, 0]
    couple = pivot_coupling[0, 0]
    pivots = inverse.shape[0]
    half_pb = pivots // 2
    fronts = lax.axis_size("front")
    leaf_index = lax.axis_index("leaf")
    side_count = right_sides.shape[0]
    carried = jnp.zeros((side_count, pivots), jnp.float32)
    weighted = []
    for level_index in range(LEVELS):
        group_width = 1 << level_index
        front_span = fronts * pivots * group_width
        column_start = fronts * pivots * (group_width - 1)
        inverse_rows = inverse[:, column_start : column_start + front_span]
        own_side = right_sides[:, level_index * pivots : (level_index + 1) * pivots] - carried
        gathered = group_gather(own_side, level_index, leaf_index)
        solved = lax.dot_general(
            gathered,
            inverse_rows,
            (((1,), (1,)), ((), ())),
            precision=exact_mode,
            preferred_element_type=jnp.float32,
        )
        weighted.append(
            pivot_solve(
                solved,
                pivot_diag[level_index * pivots : (level_index + 1) * pivots],
                couple[level_index * half_pb : (level_index + 1) * half_pb],
                pivot_kinds[level_index * half_pb : (level_index + 1) * half_pb],
            )
        )
        if level_index + 1 < LEVELS:
            update_len = 2 * pivots * group_width
            update_start = 2 * pivots * (group_width - 1)
            block_count = update_len // BLOCK
            target_start = update_start // BLOCK
            onehot_table = block_table(
                targets[target_start : target_start + block_count], 2 * front_span // BLOCK
            )
            update_part = jnp.dot(
                solved,
                update_rows[:, update_start : update_start + update_len],
                precision=exact_mode,
                preferred_element_type=jnp.float32,
            )
            spread = jnp.einsum(
                "rkc,kt->rtc",
                update_part.reshape(side_count, block_count, BLOCK),
                onehot_table,
                precision=exact_mode,
            ).reshape(side_count, 2 * front_span)
            carried = group_scatter(spread, level_index + 1, leaf_index)
    answers = [None] * LEVELS
    parent_full = None
    for level_index in reversed(range(LEVELS)):
        group_width = 1 << level_index
        front_span = fronts * pivots * group_width
        column_start = fronts * pivots * (group_width - 1)
        inverse_rows = inverse[:, column_start : column_start + front_span]
        target = weighted[level_index]
        if level_index + 1 < LEVELS:
            update_len = 2 * pivots * group_width
            update_start = 2 * pivots * (group_width - 1)
            block_count = update_len // BLOCK
            target_start = update_start // BLOCK
            onehot_table = block_table(
                targets[target_start : target_start + block_count], 2 * front_span // BLOCK
            )
            chosen = jnp.einsum(
                "rtc,kt->rkc",
                parent_full.reshape(side_count, -1, BLOCK),
                onehot_table,
                precision=exact_mode,
            ).reshape(side_count, update_len)
            target = target - lax.dot_general(
                chosen,
                update_rows[:, update_start : update_start + update_len],
                (((1,), (1,)), ((), ())),
                precision=exact_mode,
                preferred_element_type=jnp.float32,
            )
        partial_terms = jnp.dot(
            target, inverse_rows, precision=exact_mode, preferred_element_type=jnp.float32
        )
        answers[level_index] = group_scatter(partial_terms, level_index, leaf_index)
        if level_index > 0:
            parent_full = group_gather(answers[level_index], level_index, leaf_index)
    result = jnp.concatenate(answers, 1)
    return result[None, None]


def solution(mesh):
    in_specs = (
        P("leaf", "front", None, None),
        P("leaf", "front", None, None),
        P("leaf", "front", None, None),
        P("leaf", None),
        P("leaf", "front", None),
        P("leaf", "front", None),
        P("leaf", "front", None),
    )
    out_specs = P("leaf", "front", None, None)
    return jax.shard_map(
        per_device, mesh=mesh, in_specs=in_specs, out_specs=out_specs, check_vma=False
    )
```

profile of v0, /device:TPU:0, one launch (start us, length us, event | category | flops | bytes accessed | tf_op | source)
XLA Modules:
  0.0 434.3 jit_solution(10826343033905114720)
XLA Ops:
  7.4 6.8 %all_gather.21 = f32[96,512]{1,0:T(8,128)S(1)} all-gather(f32[96,128]{1,0:T(8,128)S(1)} %slice.301), channel_id=1, replica_groups=mesh['leaf'=8,'front'=4] {'front'}, dimensions={1}, use_global_device_ids=true | all-gather | bytes 245760 | tf_op jit(solution)/shard_map/all_gather | solution.py:35
  18.9 22.3 %reduce-scatter.8.cloned.1.call-done = f32[96,256]{1,0:T(8,128)} async-done(((f32[96,1024]{1,0:T(8,128)}), f32[96,256]{1,0:T(8,128)}) %reduce-scatter.8.cloned.1.call-update) | async-done | bytes 98320 | tf_op jit(solution)/shard_map/reduce_scatter | solution.py:39
  51.2 6.1 %all_gather.22 = f32[96,1024]{1,0:T(8,128)S(1)} all-gather(f32[96,256]{1,0:T(8,128)S(1)} %maximum_select_fusion.6), channel_id=1, replica_groups=mesh['leaf'=8,'front'=4] {'front'}, dimensions={1}, use_global_device_ids=true | all-gather | bytes 491520 | tf_op jit(solution)/shard_map/all_gather | solution.py:35
  61.3 23.6 %reduce-scatter.10.cloned.1.call-done = f32[96,512]{1,0:T(8,128)} async-done(((f32[96,2048]{1,0:T(8,128)}), f32[96,512]{1,0:T(8,128)}) %reduce-scatter.10.cloned.1.call-update) | async-done | bytes 196624 | tf_op jit(solution)/shard_map/reduce_scatter | solution.py:39
  104.5 7.5 %all_gather.23 = f32[96,2048]{1,0:T(8,128)S(1)} all-gather(f32[96,512]{1,0:T(8,128)S(1)} %maximum_select_fusion.2), channel_id=1, replica_groups=mesh['leaf'=8,'front'=4] {'front'}, dimensions={1}, use_global_device_ids=true | all-gather | bytes 983040 | tf_op jit(solution)/shard_map/all_gather | solution.py:35
  118.2 29.2 %reduce-scatter.12.cloned.1.call-done = f32[96,1024]{1,0:T(8,128)} async-done(((f32[96,4096]{1,0:T(8,128)}), f32[96,1024]{1,0:T(8,128)}) %reduce-scatter.12.cloned.1.call-update) | async-done | bytes 393232 | tf_op jit(solution)/shard_map/reduce_scatter | solution.py:39
  150.9 9.2 %collective-permute-done.6 = f32[96,512]{1,0:T(8,128)S(1)} collective-permute-done((f32[96,512]{1,0:T(8,128)S(1)}, f32[96,512]{1,0:T(8,128)S(1)}, u32[]{:S(2)}, u32[]{:S(2)}) %collective-permute-start.6) | collective-permute-done | bytes 196640 | tf_op jit(solution)/shard_map/ppermute | solution.py:20
  161.7 4.1 collective-permute-done.7
  174.9 5.6 %collective-permute-done.10 = f32[96,256]{1,0:T(8,128)S(1)} collective-permute-done((f32[96,256]{1,0:T(8,128)S(1)}, f32[96,256]{1,0:T(8,128)S(1)}, u32[]{:S(2)}, u32[]{:S(2)}) %collective-permute-start.10) | collective-permute-done | bytes 98336 | tf_op jit(solution)/shard_map/ppermute | solution.py:20
  182.3 6.0 %collective-permute-done.11 = f32[96,512]{1,0:T(8,128)S(1)} collective-permute-done((f32[96,512]{1,0:T(8,128)S(1)}, f32[96,512]{1,0:T(8,128)S(1)}, u32[]{:S(2)}, u32[]{:S(2)}) %collective-permute-start.11) | collective-permute-done | bytes 196640 | tf_op jit(solution)/shard_map/ppermute | solution.py:20
  190.9 17.5 %all-gather.3.cloned.1.call-done = f32[96,4096]{1,0:T(8,128)} async-done(((f32[96,1024]{1,0:T(8,128)}), f32[96,4096]{1,0:T(8,128)}) %all-gather.3.cloned.1.call-update) | async-done | bytes 1572880 | tf_op jit(solution)/shard_map/all_gather | solution.py:35
  208.4 4.0 fusion.2
  216.3 28.1 %reduce-scatter.14.cloned.1.call-done = f32[96,1024]{1,0:T(8,128)} async-done(((f32[96,4096]{1,0:T(8,128)}), f32[96,1024]{1,0:T(8,128)}) %reduce-scatter.14.cloned.1.call-update) | async-done | bytes 393232 | tf_op jit(solution)/shard_map/reduce_scatter | solution.py:39
  248.0 9.2 %collective-permute-done.12 = f32[96,512]{1,0:T(8,128)S(1)} collective-permute-done((f32[96,512]{1,0:T(8,128)S(1)}, f32[96,512]{1,0:T(8,128)S(1)}, u32[]{:S(2)}, u32[]{:S(2)}) %collective-permute-start.12) | collective-permute-done | bytes 196640 | tf_op jit(solution)/shard_map/ppermute | solution.py:20
  258.8 4.1 collective-permute-done.13
  271.9 5.6 %collective-permute-done.16 = f32[96,256]{1,0:T(8,128)S(1)} collective-permute-done((f32[96,256]{1,0:T(8,128)S(1)}, f32[96,256]{1,0:T(8,128)S(1)}, u32[]{:S(2)}, u32[]{:S(2)}) %collective-permute-start.16) | collective-permute-done | bytes 98336 | tf_op jit(solution)/shard_map/ppermute | solution.py:20
  279.3 6.0 %collective-permute-done.17 = f32[96,512]{1,0:T(8,128)S(1)} collective-permute-done((f32[96,512]{1,0:T(8,128)S(1)}, f32[96,512]{1,0:T(8,128)S(1)}, u32[]{:S(2)}, u32[]{:S(2)}) %collective-permute-start.17) | collective-permute-done | bytes 196640 | tf_op jit(solution)/shard_map/ppermute | solution.py:20
  286.3 19.3 %all-gather.5.cloned.1.call-done = f32[96,4096]{1,0:T(8,128)} async-done(((f32[96,1024]{1,0:T(8,128)}), f32[96,4096]{1,0:T(8,128)}) %all-gather.5.cloned.1.call-update) | async-done | bytes 1572880 | tf_op jit(solution)/shard_map/all_gather | solution.py:35
  311.5 23.3 %reduce-scatter.16.cloned.1.call-done = f32[96,512]{1,0:T(8,128)} async-done(((f32[96,2048]{1,0:T(8,128)}), f32[96,512]{1,0:T(8,128)}) %reduce-scatter.16.cloned.1.call-update) | async-done | bytes 196624 | tf_op jit(solution)/shard_map/reduce_scatter | solution.py:39
  337.3 3.1 collective-permute-done.18
  354.5 7.5 %all_gather.26 = f32[96,2048]{1,0:T(8,128)S(1)} all-gather(f32[96,512]{1,0:T(8,128)S(1)} %maximum_select_fusion.5), channel_id=1, replica_groups=mesh['leaf'=8,'front'=4] {'front'}, dimensions={1}, use_global_device_ids=true | all-gather | bytes 983040 | tf_op jit(solution)/shard_map/all_gather | solution.py:35
  365.2 22.0 %reduce-scatter.18.cloned.1.call-done = f32[96,256]{1,0:T(8,128)} async-done(((f32[96,1024]{1,0:T(8,128)}), f32[96,256]{1,0:T(8,128)}) %reduce-scatter.18.cloned.1.call-update) | async-done | bytes 98320 | tf_op jit(solution)/shard_map/reduce_scatter | solution.py:39
  397.2 6.1 %all_gather.27 = f32[96,1024]{1,0:T(8,128)S(1)} all-gather(f32[96,256]{1,0:T(8,128)S(1)} %maximum_select_fusion.11), channel_id=1, replica_groups=mesh['leaf'=8,'front'=4] {'front'}, dimensions={1}, use_global_device_ids=true | all-gather | bytes 491520 | tf_op jit(solution)/shard_map/all_gather | solution.py:35
  406.0 20.2 %reduce-scatter.20.cloned.1.call-done = f32[96,128]{1,0:T(8,128)} async-done(((f32[96,512]{1,0:T(8,128)}), f32[96,128]{1,0:T(8,128)}) %reduce-scatter.20.cloned.1.call-update) | async-done | bytes 49168 | tf_op jit(solution)/shard_map/reduce_scatter | solution.py:39
  (161 shorter events, 124.0 us)
Async XLA Ops:
  6.5 34.7 %reduce-scatter.8.cloned.1.call-start = ((), (), s32[]{:S(2)}) async-start(), calls=%async_computation.7 | async-start | bytes 491520 | tf_op jit(solution)/shard_map/reduce_scatter | solution.py:39
  18.8 66.0 %reduce-scatter.10.cloned.1.call-start = ((), (), s32[]{:S(2)}) async-start(), calls=%async_computation.8 | async-start | bytes 983040 | tf_op jit(solution)/shard_map/reduce_scatter | solution.py:39
  47.0 4.2 collective-permute-start.1
  61.2 86.1 %reduce-scatter.12.cloned.1.call-start = ((), (), s32[]{:S(2)}) async-start(), calls=%async_computation.9 | async-start | bytes 1966080 | tf_op jit(solution)/shard_map/reduce_scatter | solution.py:39
  85.8 4.7 %collective-permute-start.2 = (f32[96,256]{1,0:T(8,128)S(1)}, f32[96,256]{1,0:T(8,128)S(1)}, u32[]{:S(2)}, u32[]{:S(2)}) collective-permute-start(f32[96,256]{1,0:T(8,128)S(1)} %slice_select_fusion.5), channel_id=1, source_target_pairs={{0,8},{8,0},{4,12},{12,4},{16,24},{24,16},{20,28},{28,20},{1,9},{9... | collective-permute-start | bytes 294920 | tf_op jit(solution)/shard_map/ppermute | solution.py:20
  99.8 4.7 %collective-permute-start.5 = (f32[96,256]{1,0:T(8,128)S(1)}, f32[96,256]{1,0:T(8,128)S(1)}, u32[]{:S(2)}, u32[]{:S(2)}) collective-permute-start(f32[96,256]{1,0:T(8,128)S(1)} %maximum_select_fusion.7), channel_id=1, source_target_pairs={{0,8},{8,0},{4,12},{12,4},{16,24},{24,16},{20,28},{28,20},{1,9},{9... | collective-permute-start | bytes 294920 | tf_op jit(solution)/shard_map/ppermute | solution.py:20
  118.1 90.3 %all-gather.3.cloned.1.call-start = ((), (), s32[]{:S(2)}) async-start(), calls=%async_computation.10 | async-start | bytes 1966080 | tf_op jit(solution)/shard_map/all_gather | solution.py:35
  148.4 11.7 %collective-permute-start.6 = (f32[96,512]{1,0:T(8,128)S(1)}, f32[96,512]{1,0:T(8,128)S(1)}, u32[]{:S(2)}, u32[]{:S(2)}) collective-permute-start(f32[96,512]{1,0:T(8,128)S(1)} %slice_select_fusion.1), channel_id=1, source_target_pairs={{0,16},{16,0},{4,20},{20,4},{8,24},{24,8},{12,28},{28,12},{1,17},{... | collective-permute-start | bytes 589832 | tf_op jit(solution)/shard_map/ppermute | solution.py:20
  161.1 4.7 %collective-permute-start.7 = (f32[96,256]{1,0:T(8,128)S(1)}, f32[96,256]{1,0:T(8,128)S(1)}, u32[]{:S(2)}, u32[]{:S(2)}) collective-permute-start(f32[96,256]{1,0:T(8,128)S(1)} %slice_select_fusion.4), channel_id=1, source_target_pairs={{0,8},{8,0},{4,12},{12,4},{16,24},{24,16},{20,28},{28,20},{1,9},{9... | collective-permute-start | bytes 294920 | tf_op jit(solution)/shard_map/ppermute | solution.py:20
  165.9 4.7 %collective-permute-start.8 = (f32[96,128]{1,0:T(8,128)S(1)}, f32[96,128]{1,0:T(8,128)S(1)}, u32[]{:S(2)}, u32[]{:S(2)}) collective-permute-start(f32[96,128]{1,0:T(8,128)S(1)} %slice_select_fusion.9), channel_id=1, source_target_pairs={{0,4},{4,0},{8,12},{12,8},{16,20},{20,16},{24,28},{28,24},{1,5},{5... | collective-permute-start | bytes 147464 | tf_op jit(solution)/shard_map/ppermute | solution.py:20
  174.7 5.8 %collective-permute-start.10 = (f32[96,256]{1,0:T(8,128)S(1)}, f32[96,256]{1,0:T(8,128)S(1)}, u32[]{:S(2)}, u32[]{:S(2)}) collective-permute-start(f32[96,256]{1,0:T(8,128)S(1)} %maximum_select_fusion.8), channel_id=1, source_target_pairs={{0,8},{8,0},{4,12},{12,4},{16,24},{24,16},{20,28},{28,20},{1,9},{9... | collective-permute-start | bytes 294920 | tf_op jit(solution)/shard_map/ppermute | solution.py:20
  180.5 7.7 %collective-permute-start.11 = (f32[96,512]{1,0:T(8,128)S(1)}, f32[96,512]{1,0:T(8,128)S(1)}, u32[]{:S(2)}, u32[]{:S(2)}) collective-permute-start(f32[96,512]{1,0:T(8,128)S(1)} %maximum_select_fusion.3), channel_id=1, source_target_pairs={{0,16},{16,0},{4,20},{20,4},{8,24},{24,8},{12,28},{28,12},{1,17},{... | collective-permute-start | bytes 589832 | tf_op jit(solution)/shard_map/ppermute | solution.py:20
  189.1 55.4 %reduce-scatter.14.cloned.1.call-start = ((), (), s32[]{:S(2)}) async-start(), calls=%async_computation.11 | async-start | bytes 1966080 | tf_op jit(solution)/shard_map/reduce_scatter | solution.py:39
  216.3 89.2 %all-gather.5.cloned.1.call-start = ((), (), s32[]{:S(2)}) async-start(), calls=%async_computation.12 | async-start | bytes 1966080 | tf_op jit(solution)/shard_map/all_gather | solution.py:35
  245.5 11.7 %collective-permute-start.12 = (f32[96,512]{1,0:T(8,128)S(1)}, f32[96,512]{1,0:T(8,128)S(1)}, u32[]{:S(2)}, u32[]{:S(2)}) collective-permute-start(f32[96,512]{1,0:T(8,128)S(1)} %slice_select_fusion), channel_id=1, source_target_pairs={{0,16},{16,0},{4,20},{20,4},{8,24},{24,8},{12,28},{28,12},{1,17},{... | collective-permute-start | bytes 589832 | tf_op jit(solution)/shard_map/ppermute | solution.py:20
  258.2 4.7 %collective-permute-start.13 = (f32[96,256]{1,0:T(8,128)S(1)}, f32[96,256]{1,0:T(8,128)S(1)}, u32[]{:S(2)}, u32[]{:S(2)}) collective-permute-start(f32[96,256]{1,0:T(8,128)S(1)} %slice_select_fusion.3), channel_id=1, source_target_pairs={{0,8},{8,0},{4,12},{12,4},{16,24},{24,16},{20,28},{28,20},{1,9},{9... | collective-permute-start | bytes 294920 | tf_op jit(solution)/shard_map/ppermute | solution.py:20
  263.0 4.7 %collective-permute-start.14 = (f32[96,128]{1,0:T(8,128)S(1)}, f32[96,128]{1,0:T(8,128)S(1)}, u32[]{:S(2)}, u32[]{:S(2)}) collective-permute-start(f32[96,128]{1,0:T(8,128)S(1)} %slice_select_fusion.8), channel_id=1, source_target_pairs={{0,4},{4,0},{8,12},{12,8},{16,20},{20,16},{24,28},{28,24},{1,5},{5... | collective-permute-start | bytes 147464 | tf_op jit(solution)/shard_map/ppermute | solution.py:20
  271.8 5.8 %collective-permute-start.16 = (f32[96,256]{1,0:T(8,128)S(1)}, f32[96,256]{1,0:T(8,128)S(1)}, u32[]{:S(2)}, u32[]{:S(2)}) collective-permute-start(f32[96,256]{1,0:T(8,128)S(1)} %maximum_select_fusion.9), channel_id=1, source_target_pairs={{0,8},{8,0},{4,12},{12,4},{16,24},{24,16},{20,28},{28,20},{1,9},{9... | collective-permute-start | bytes 294920 | tf_op jit(solution)/shard_map/ppermute | solution.py:20
  277.6 7.7 %collective-permute-start.17 = (f32[96,512]{1,0:T(8,128)S(1)}, f32[96,512]{1,0:T(8,128)S(1)}, u32[]{:S(2)}, u32[]{:S(2)}) collective-permute-start(f32[96,512]{1,0:T(8,128)S(1)} %maximum_select_fusion.4), channel_id=1, source_target_pairs={{0,16},{16,0},{4,20},{20,4},{8,24},{24,8},{12,28},{28,12},{1,17},{... | collective-permute-start | bytes 589832 | tf_op jit(solution)/shard_map/ppermute | solution.py:20
  286.1 48.7 %reduce-scatter.16.cloned.1.call-start = ((), (), s32[]{:S(2)}) async-start(), calls=%async_computation.13 | async-start | bytes 983040 | tf_op jit(solution)/shard_map/reduce_scatter | solution.py:39
  311.4 75.8 %reduce-scatter.18.cloned.1.call-start = ((), (), s32[]{:S(2)}) async-start(), calls=%async_computation.14 | async-start | bytes 491520 | tf_op jit(solution)/shard_map/reduce_scatter | solution.py:39
  335.8 4.7 %collective-permute-start.18 = (f32[96,256]{1,0:T(8,128)S(1)}, f32[96,256]{1,0:T(8,128)S(1)}, u32[]{:S(2)}, u32[]{:S(2)}) collective-permute-start(f32[96,256]{1,0:T(8,128)S(1)} %slice_select_fusion.2), channel_id=1, source_target_pairs={{0,8},{8,0},{4,12},{12,4},{16,24},{24,16},{20,28},{28,20},{1,9},{9... | collective-permute-start | bytes 294920 | tf_op jit(solution)/shard_map/ppermute | solution.py:20
  349.7 4.7 %collective-permute-start.21 = (f32[96,256]{1,0:T(8,128)S(1)}, f32[96,256]{1,0:T(8,128)S(1)}, u32[]{:S(2)}, u32[]{:S(2)}) collective-permute-start(f32[96,256]{1,0:T(8,128)S(1)} %maximum_select_fusion.10), channel_id=1, source_target_pairs={{0,8},{8,0},{4,12},{12,4},{16,24},{24,16},{20,28},{28,20},{1,9},{9... | collective-permute-start | bytes 294920 | tf_op jit(solution)/shard_map/ppermute | solution.py:20
  365.2 61.1 %reduce-scatter.20.cloned.1.call-start = ((), (), s32[]{:S(2)}) async-start(), calls=%async_computation.15 | async-start | bytes 245760 | tf_op jit(solution)/shard_map/reduce_scatter | solution.py:39
  (16 other events, 383.4 us)
Sparse Core Ops, SparseCore 0:
  19.0 22.2 reduce-scatter.7
  61.3 23.4 reduce-scatter.9
  118.2 29.1 reduce-scatter.11
  189.2 19.2 all-gather.2
  216.4 27.9 reduce-scatter.13
  286.3 19.2 all-gather.4
  311.6 23.1 reduce-scatter.15
  365.3 21.8 reduce-scatter.17
  406.2 20.0 reduce-scatter.19
where the time goes:
time: 435 us; the launch traced here: 434 us
  waiting for transfers between devices  299 us (69%)
  starting transfers between devices  34.9 us (8%)
  blocking collectives  34 us (8%)
  matrix products  26 us (6%)
  other arithmetic  16.9 us (4%)
  between operations  13.6 us (3%)
  local copies, waits for them, and re-layouts  9.63 us (2%)
    reduce_scatter x7, waiting for transfers between devices, group_scatter(): lax.psum_scatter(partial_terms, 'front', scatter_dimension=1, tiled=True)  169 us
    ppermute x24, waiting for transfers between devices, from_partner(): return lax.ppermute(block, axis, route)  93.4 us
    all_gather x2, waiting for transfers between devices, group_gather(): return lax.all_gather(joined, 'front', axis=1, tiled=True)  36.8 us
    ppermute x24, starting transfers between devices, from_partner(): return lax.ppermute(block, axis, route)  34.4 us
    all_gather x5, blocking collectives, group_gather(): return lax.all_gather(joined, 'front', axis=1, tiled=True)  34 us
    dot_general x4, matrix products, per_device(): jnp.dot(target, inverse_rows, precision=exact_mode, preferred_element_typ...  10.1 us
    dot_general x4, matrix products, per_device(): lax.dot_general(gathered, inverse_rows, (((1,), (1,)), ((), ())), precisi...  9.35 us
  transfers between devices with their start and end apart: 33, of which 33 were waited for; matrix products, arithmetic and copies ran while one was open for 1% of the time, Pallas kernels for 0%

commit v1 on v0

v1 whole, which is shorter than its diff:
```python
import functools

import jax
import jax.numpy as jnp
from jax import lax
from jax.experimental import pallas as pl
from jax.experimental.pallas import tpu as pltpu
from jax.sharding import PartitionSpec as P

LEVELS = 4
BLOCK = 128
MESH = pl.DeviceIdType.MESH
F32 = jnp.float32
BF16 = jnp.bfloat16


def flip(value, mask):
    result = value
    bit = 0
    while mask >> bit:
        if mask >> bit & 1:
            unit = 1 << bit
            result = result + (1 - 2 * lax.rem(lax.div(value, unit), 2)) * unit
        bit += 1
    return result


def split(values):
    high = values.astype(BF16)
    return high, (values - high.astype(F32)).astype(BF16)


def rows_of(values):
    high, low = split(values)
    return jnp.concatenate([high, low], 0)


def square_of(values):
    high, low = split(values)
    return jnp.concatenate(
        [jnp.concatenate([high, high], 1), jnp.concatenate([low, low], 1)], 0
    )


def along_columns(stacked, matrix):
    return lax.dot_general(
        stacked, matrix, (((1,), (1,)), ((), ())), preferred_element_type=F32
    )


def fold(product, sides, width):
    return (product[:sides, :width] + product[sides:, :width]) + (
        product[:sides, width:] + product[sides:, width:]
    )


def across(square, matrix, sides):
    product = jnp.dot(square, matrix, preferred_element_type=F32)
    return product[:sides] + product[sides:]


class Plan:
    def __init__(self, fronts, sides):
        self.fronts, self.sides = fronts, sides
        half = sides // 2
        self.gathers = {}
        self.scatters = {}
        for level in range(LEVELS):
            self.gathers["rhs", level] = (level, sides)
            self.scatters["out", level] = (level, sides)
        for level in range(LEVELS - 1):
            self.scatters["up", level] = (level, half)
            self.gathers["up", level] = (level + 1, half)
            self.scatters["down", level] = (level + 1, half)
            self.gathers["down", level] = (level, half)

    def size(self, level):
        return self.fronts << level

    def pre(self, level):
        return level >= 2


def kernel(plan, pivots, *refs):
    (
        rhs_ref,
        inverse_hbm,
        update_hbm,
        targets_ref,
        pairs_ref,
        diagonal_ref,
        coupling_ref,
        out_ref,
        inverse_raw,
        update_raw,
        inverse_split,
        update_split,
        targets_far,
        targets_smem,
        load_sem,
        targets_send,
        targets_recv,
        gather_send,
        gather_recv,
        scatter_send,
        scatter_recv,
        *buffers,
    ) = refs
    sides, fronts = plan.sides, plan.fronts
    half = sides // 2
    nx = fronts // 2
    leaf = lax.axis_index("leaf")
    front = lax.axis_index("front")
    core, column = lax.rem(front, 2), lax.div(front, 2)

    gather_keys = list(plan.gathers)
    scatter_keys = list(plan.scatters)
    gather_buffer, part, landed, first = {}, {}, {}, {}
    buffers = list(buffers)
    for key in gather_keys:
        gather_buffer[key] = buffers.pop(0)
    for key in scatter_keys:
        part[key] = buffers.pop(0)
        landed[key] = buffers.pop(0)
        if plan.pre(plan.scatters[key][0]):
            first[key] = buffers.pop(0)

    def rank(level):
        return core * (nx << level) + column * (1 << level) + lax.rem(leaf, 1 << level)

    def peer(level, mask):
        return (
            flip(leaf, mask % (1 << level)),
            flip(column, (mask >> level) % nx) * 2 + flip(core, mask // (nx << level)),
        )

    def slot_block(level, slot):
        slot_core, rest = divmod(slot, nx << level)
        slot_column, offset = divmod(rest, 1 << level)
        return ((slot_column * 2 + slot_core) << level) + offset

    def slot_of(level, block):
        index, offset = divmod(block, 1 << level)
        return (index % 2) * (nx << level) + (index // 2) * (1 << level) + offset

    sends = []

    def send(source, target, send_sem, recv_sem, device):
        pltpu.make_async_remote_copy(
            source, target, send_sem, recv_sem, device_id=device, device_id_type=MESH
        ).start()

    def wait_recv(buffer, count, send_sem, recv_sem):
        span = buffer.at[pl.ds(0, count)]
        pltpu.make_async_remote_copy(
            span, span, send_sem, recv_sem, device_id=peer(0, 1), device_id_type=MESH
        ).wait_recv()

    def wait_send(buffer, count, send_sem, recv_sem):
        span = buffer.at[pl.ds(0, count)]
        pltpu.make_async_remote_copy(
            span, span, send_sem, recv_sem, device_id=peer(0, 1), device_id_type=MESH
        ).wait_send()

    def gather_start(key):
        level, _ = plan.gathers[key]
        buffer, index = gather_buffer[key], gather_keys.index(key)
        mine = rank(level)
        sems = gather_send.at[index, 0], gather_recv.at[index, 0]
        for mask in range(1, nx << level):
            send(buffer.at[mine], buffer.at[mine], *sems, peer(level, mask))
        sends.append((buffer, (nx << level) - 1, *sems))

    def gather_forward(key):
        level, _ = plan.gathers[key]
        buffer, index = gather_buffer[key], gather_keys.index(key)
        count = nx << level
        wait_recv(buffer, count - 1, gather_send.at[index, 0], gather_recv.at[index, 0])
        span = buffer.at[pl.ds(core * count, count)]
        sems = gather_send.at[index, 1], gather_recv.at[index, 1]
        send(span, span, *sems, peer(level, count))
        sends.append((buffer, count, *sems))

    def gather_finish(key):
        level, _ = plan.gathers[key]
        index = gather_keys.index(key)
        wait_recv(
            gather_buffer[key], nx << level, gather_send.at[index, 1], gather_recv.at[index, 1]
        )

    def scatter_start(key):
        level, _ = plan.scatters[key]
        index = scatter_keys.index(key)
        count = nx << level
        if plan.pre(level):
            sems = scatter_send.at[index, 0], scatter_recv.at[index, 0]
            send(
                part[key].at[pl.ds((1 - core) * count, count)], first[key], *sems, peer(level, count)
            )
            sends.append((part[key], count, *sems))
        else:
            scatter_spread(key, 2 * count)

    def scatter_spread(key, count):
        level, _ = plan.scatters[key]
        index = scatter_keys.index(key)
        mine = rank(level)
        sems = scatter_send.at[index, 1], scatter_recv.at[index, 1]
        for mask in range(1, count):
            send(
                part[key].at[flip(mine, mask)], landed[key].at[mask - 1], *sems, peer(level, mask)
            )
        sends.append((part[key], count - 1, *sems))

    def scatter_middle(key):
        level, _ = plan.scatters[key]
        index = scatter_keys.index(key)
        count = nx << level
        if plan.pre(level):
            wait_recv(first[key], count, scatter_send.at[index, 0], scatter_recv.at[index, 0])
            span = pl.ds(core * count, count)
            part[key][span] = part[key][span] + first[key][...]
            scatter_spread(key, count)

    def scatter_finish(key):
        level, _ = plan.scatters[key]
        index = scatter_keys.index(key)
        count = (nx << level) if plan.pre(level) else fronts << level
        wait_recv(landed[key], count - 1, scatter_send.at[index, 1], scatter_recv.at[index, 1])
        total = part[key][rank(level)]
        for place in range(count - 1):
            total = total + landed[key][place]
        return total

    def column_start(level):
        return fronts * pivots * ((1 << level) - 1)

    def update_start(level):
        return 2 * pivots * ((1 << level) - 1)

    loads = []
    for level in range(LEVELS):
        cols = pl.ds(column_start(level), (fronts * pivots) << level)
        loads.append(
            pltpu.make_async_copy(
                inverse_hbm.at[0, 0, :, cols], inverse_raw.at[:, cols], load_sem.at[level]
            )
        )
    loads.append(pltpu.make_async_copy(update_hbm.at[0, 0], update_raw, load_sem.at[LEVELS]))
    loads[0].start()
    loads[LEVELS].start()
    for level in range(1, LEVELS):
        loads[level].start()

    for level in range(LEVELS):
        gather_buffer["rhs", level][rank(level)] = rhs_ref[
            0, 0, :, level * pivots : (level + 1) * pivots
        ]

    barrier = pltpu.get_barrier_semaphore()
    everyone = plan.size(LEVELS - 1)
    for mask in range(1, everyone):
        pl.semaphore_signal(
            barrier, inc=1, device_id=peer(LEVELS - 1, mask), device_id_type=MESH
        )
    pl.semaphore_wait(barrier, everyone - 1)

    gather_start(("rhs", 0))
    for level in range(LEVELS - 1):
        send(
            targets_ref,
            targets_far.at[level],
            targets_send.at[level],
            targets_recv.at[level],
            (flip(leaf, 1 << level), front),
        )
    gather_start(("rhs", 1))

    def prepare(level):
        loads[level].wait()
        for block in range(column_start(level) // BLOCK, column_start(level + 1) // BLOCK):
            high, low = split(inverse_raw[:, block * BLOCK : (block + 1) * BLOCK])
            inverse_split[block, :pivots] = high
            inverse_split[block, pivots:] = low

    def inverse_columns(start, stop):
        blocks = range(start // BLOCK, stop // BLOCK)
        return jnp.concatenate([inverse_split[block] for block in blocks], 1)

    prepare(0)
    loads[LEVELS].wait()
    high, low = split(update_raw[...])
    update_split[:pivots] = high
    update_split[pivots:] = low

    count = diagonal_ref.shape[2]
    from_pair = (
        lax.div(lax.broadcasted_iota(jnp.int32, (count // 2, count), 1), 2)
        == lax.broadcasted_iota(jnp.int32, (count // 2, count), 0)
    ).astype(F32)
    pair_rows = jnp.concatenate(
        [
            jnp.broadcast_to(coupling_ref[0], (8, count // 2)),
            jnp.broadcast_to(pairs_ref[0].astype(F32), (8, count // 2)),
        ],
        0,
    )
    repeated = jnp.dot(
        pair_rows, from_pair, precision=lax.Precision.HIGHEST, preferred_element_type=F32
    )
    couple, flags = repeated[:8], repeated[8:] > 0.5
    diagonal = jnp.broadcast_to(diagonal_ref[0], (8, count))

    def swap(values):
        width = values.shape[1]
        even = lax.rem(lax.broadcasted_iota(jnp.int32, values.shape, 1), 2) == 0
        return jnp.where(
            even, pltpu.roll(values, width - 1, 1), pltpu.roll(values, 1, 1)
        )

    other_diagonal = swap(diagonal)
    determinant = diagonal * other_diagonal - couple * couple
    straight = jnp.where(flags, other_diagonal / determinant, 1.0 / diagonal)[:1]
    crossed = jnp.where(flags, -couple / determinant, 0.0)[:1]

    def pivot_solve(solved, level):
        span = slice(level * pivots, (level + 1) * pivots)
        return solved * straight[:, span] + swap(solved) * crossed[:, span]

    for level in range(LEVELS - 1):
        pltpu.make_async_remote_copy(
            targets_ref,
            targets_far.at[level],
            targets_send.at[level],
            targets_recv.at[level],
            device_id=(flip(leaf, 1 << level), front),
            device_id_type=MESH,
        ).wait()
    lists = [targets_ref] + [targets_far.at[level] for level in range(LEVELS - 1)]
    for index, source in enumerate(lists):
        pltpu.make_async_copy(source, targets_smem.at[index], load_sem.at[LEVELS + 1]).start()
        pltpu.make_async_copy(source, targets_smem.at[index], load_sem.at[LEVELS + 1]).wait()

    def block_count(level):
        return 2 * pivots * (1 << level) // BLOCK

    def chosen_columns(level, child, index):
        place = update_start(level) // BLOCK + index
        upper = lax.rem(lax.div(leaf, 1 << level), 2)
        near, far = targets_smem[0, 0, place], targets_smem[level + 1, 0, place]
        block = near + (far - near) * (upper + child - 2 * upper * child)
        return inverse_split[column_start(level + 1) // BLOCK + block]

    def known_part(level):
        buffer = gather_buffer["rhs", level]
        product = None
        step = 2 if level else 1
        for slot in range(0, plan.size(level), step):
            start = column_start(level) + slot_block(level, slot) * pivots
            values = jnp.concatenate([buffer[slot + i] for i in range(step)], 1)
            term = along_columns(
                rows_of(values), inverse_columns(start, start + step * pivots)
            )
            product = term if product is None else product + term
        return product

    def block_at(buffer, level, child, index, parent):
        halves = []
        for place in (2 * index, 2 * index + 1):
            slot = slot_of(level, place)
            if parent:
                rank_core, rest = divmod(slot, nx << level)
                rank_column, offset = divmod(rest, 1 << level)
                slot = (
                    rank_core * (nx << (level + 1))
                    + rank_column * (1 << (level + 1))
                    + (child << level)
                    + offset
                )
            halves.append(slot)
        return halves

    weighted = []
    gather_forward(("rhs", 0))
    gather_finish(("rhs", 0))
    product = known_part(0)
    for level in range(LEVELS):
        if level:
            below = level - 1
            key = ("up", below)
            gather_finish(key)
            buffer = gather_buffer[key]
            for child in range(2):
                for index in range(0, block_count(below), 2):
                    values, matrices = [], []
                    for i in (index, index + 1):
                        low_slot, high_slot = block_at(buffer, below, child, i, True)
                        values.append(
                            jnp.concatenate([buffer[low_slot], buffer[high_slot]], 0)
                        )
                        matrices.append(chosen_columns(below, child, i))
                    product = product - along_columns(
                        rows_of(jnp.concatenate(values, 1)), jnp.concatenate(matrices, 1)
                    )
        solved = fold(product, sides, pivots)
        weighted.append(pivot_solve(solved, level))
        if level + 1 < LEVELS:
            key = ("up", level)
            start = update_start(level)
            blocks = block_count(level)
            partial = across(
                square_of(solved), update_split[:, start : start + blocks * BLOCK], sides
            )
            for index in range(blocks):
                for i, slot in enumerate(block_at(None, level, 0, index, False)):
                    part[key][slot] = partial[
                        i * half : (i + 1) * half, index * BLOCK : (index + 1) * BLOCK
                    ]
            scatter_start(key)
            prepare(level + 1)
            scatter_middle(key)
            if level == 0:
                gather_forward(("rhs", 1))
            total = scatter_finish(key)
            gather_buffer[key][rank(level + 1)] = total
            gather_start(key)
            if level + 2 < LEVELS:
                gather_start(("rhs", level + 2))
            if level:
                gather_forward(("rhs", level + 1))
            gather_finish(("rhs", level + 1))
            product = known_part(level + 1)
            gather_forward(key)

    for level in reversed(range(LEVELS)):
        target = weighted[level]
        if level + 1 < LEVELS:
            key = ("down", level)
            gather_finish(key)
            buffer = gather_buffer[key]
            product = None
            for index in range(0, block_count(level), 2):
                values = []
                for i in (index, index + 1):
                    low_slot, high_slot = block_at(buffer, level, 0, i, False)
                    values.append(jnp.concatenate([buffer[low_slot], buffer[high_slot]], 0))
                start = update_start(level) + index * BLOCK
                term = along_columns(
                    rows_of(jnp.concatenate(values, 1)),
                    update_split[:, start : start + 2 * BLOCK],
                )
                product = term if product is None else product + term
            target = target - fold(product, sides, pivots)
        square = square_of(target)
        if level:
            key = ("down", level - 1)
            for child in range(2):
                for index in range(0, block_count(level - 1), 2):
                    matrix = jnp.concatenate(
                        [chosen_columns(level - 1, child, i) for i in (index, index + 1)], 1
                    )
                    partial = across(square, matrix, sides)
                    for j in range(2):
                        places = block_at(None, level - 1, child, index + j, True)
                        for i, slot in enumerate(places):
                            part[key][slot] = partial[
                                i * half : (i + 1) * half, j * BLOCK : (j + 1) * BLOCK
                            ]
            scatter_start(key)
        out_key = ("out", level)
        step = 2 if level else 1
        for slot in range(0, plan.size(level), step):
            start = column_start(level) + slot_block(level, slot) * pivots
            partial = across(square, inverse_columns(start, start + step * pivots), sides)
            for i in range(step):
                part[out_key][slot + i] = partial[:, i * pivots : (i + 1) * pivots]
        if level:
            scatter_middle(key)
            total = scatter_finish(key)
            gather_buffer[key][rank(level - 1)] = total
            gather_start(key)
            scatter_start(out_key)
            gather_forward(key)
            scatter_middle(out_key)
        else:
            scatter_start(out_key)
            scatter_middle(out_key)
    for level in reversed(range(LEVELS)):
        out_ref[0, 0, :, level * pivots : (level + 1) * pivots] = scatter_finish(("out", level))
    for item in sends:
        wait_send(*item)


def per_device(*arguments):
    (
        right_side,
        factor_inverse,
        update_panel,
        update_targets,
        pivot_pairs,
        pivot_diagonal,
        pivot_coupling,
    ) = arguments
    pivots = factor_inverse.shape[2]
    sides = right_side.shape[2]
    fronts = lax.axis_size("front")
    plan = Plan(fronts, sides)
    nx = fronts // 2
    targets = jnp.pad(update_targets, ((0, 7), (0, BLOCK - update_targets.shape[1])))
    buffers = []
    for level, rows in plan.gathers.values():
        buffers.append(pltpu.VMEM((plan.size(level), rows, pivots), F32))
    for level, rows in plan.scatters.values():
        buffers.append(pltpu.VMEM((plan.size(level), rows, pivots), F32))
        buffers.append(pltpu.VMEM((plan.size(level), rows, pivots), F32))
        if plan.pre(level):
            buffers.append(pltpu.VMEM((nx << level, rows, pivots), F32))
    vmem = pl.BlockSpec(memory_space=pltpu.VMEM)
    hbm = pl.BlockSpec(memory_space=pl.ANY)
    dma = pltpu.SemaphoreType.DMA
    return pl.pallas_call(
        functools.partial(kernel, plan, pivots),
        out_shape=jax.ShapeDtypeStruct(right_side.shape, F32),
        in_specs=[vmem, hbm, hbm, vmem, vmem, vmem, vmem],
        out_specs=vmem,
        scratch_shapes=[
            pltpu.VMEM(factor_inverse.shape[2:], F32),
            pltpu.VMEM(update_panel.shape[2:], F32),
            pltpu.VMEM((factor_inverse.shape[3] // BLOCK, 2 * pivots, BLOCK), BF16),
            pltpu.VMEM((2 * pivots, update_panel.shape[3]), BF16),
            pltpu.VMEM((LEVELS - 1,) + targets.shape, jnp.int32),
            pltpu.SMEM((LEVELS,) + targets.shape, jnp.int32),
            dma((LEVELS + 2,)),
            dma((LEVELS - 1,)),
            dma((LEVELS - 1,)),
            dma((len(plan.gathers), 2)),
            dma((len(plan.gathers), 2)),
            dma((len(plan.scatters), 2)),
            dma((len(plan.scatters), 2)),
            *buffers,
        ],
        compiler_params=pltpu.CompilerParams(collective_id=0, has_side_effects=True),
    )(
        right_side,
        factor_inverse,
        update_panel,
        targets,
        pivot_pairs,
        pivot_diagonal,
        pivot_coupling,
    )


def solution(mesh):
    in_specs = (
        P("leaf", "front", None, None),
        P("leaf", "front", None, None),
        P("leaf", "front", None, None),
        P("leaf", None),
        P("leaf", "front", None),
        P("leaf", "front", None),
        P("leaf", "front", None),
    )
    out_specs = P("leaf", "front", None, None)
    return jax.shard_map(
        per_device, mesh=mesh, in_specs=in_specs, out_specs=out_specs, check_vma=False
    )
```

time: 435 us -> 116 us (0.27)
  waiting for transfers between devices: 299 us -> 0 us
  Pallas kernels: 0 us -> 111 us
  starting transfers between devices: 34.9 us -> 0 us
  blocking collectives: 34 us -> 0 us
  matrix products: 26 us -> 0 us
  other arithmetic: 16.9 us -> 0 us
  between operations: 13.6 us -> 0.01 us
  local copies, waits for them, and re-layouts: 9.63 us -> 2.87 us
    reduce_scatter x7 -> x0, waiting for transfers between devices: 169 us -> none  [group_scatter(): lax.psum_scatter(partial_terms, 'front', scatter_dimension=1, tiled=True)]
    pallas_call x0 -> x1, Pallas kernels: none -> 111 us  [per_device(): pl.pallas_call(functools.partial(kernel, plan, pivots), out_shape=jax.Sha...]
    ppermute x24 -> x0, waiting for transfers between devices: 93.4 us -> none  [from_partner(): return lax.ppermute(block, axis, route)]
    all_gather x2 -> x0, waiting for transfers between devices: 36.8 us -> none  [group_gather(): return lax.all_gather(joined, 'front', axis=1, tiled=True)]
    ppermute x24 -> x0, starting transfers between devices: 34.4 us -> none  [from_partner(): return lax.ppermute(block, axis, route)]
    all_gather x5 -> x0, blocking collectives: 34 us -> none  [group_gather(): return lax.all_gather(joined, 'front', axis=1, tiled=True)]
    dot_general x20 -> x0, matrix products: 26 us -> none  [the longest x4 10.1 us: per_device(): jnp.dot(target, inverse_rows, precision=exact_mode, preferred_element_typ...]
    select_n x26 -> x0, other arithmetic: 9.17 us -> none  [the longest x12 5.72 us: group_scatter(): sent_half = jnp.where(is_upper, lower_half, higher)]
  transfers between devices with their start and end apart: 33 -> 0, of which waited for: 33 -> 0; matrix products, arithmetic and copies ran while one was open for 1% -> 0% of each run, Pallas kernels for 0% -> 0%
where the time goes in v1:
time: 116 us; the launch traced here: 114 us
  Pallas kernels  111 us (96%)
  local copies, waits for them, and re-layouts  2.87 us (2%)
    pallas_call x1, Pallas kernels, per_device(): pl.pallas_call(functools.partial(kernel, plan, pivots), out_shape=jax.Sha...  111 us

profile of v1, /device:TPU:0, one launch (start us, length us, event | category | flops | bytes accessed | tf_op | source)
XLA Modules:
  0.0 114.2 jit_solution(7219947964630518851)
XLA Ops:
  0.0 1.3 %pad.4.refs_3_ = s32[8,128]{1,0:T(8,128)} pad(s32[1,14]{1,0:T(1,128)} %param.10, s32[]{:T(128)} %constant.0.clone.1), padding=0_7x0_114 | pad | bytes 4156 | tf_op jit(solution)/shard_map/jit(_pad)/pad | solution.py:509
  1.3 111.3 %shard_map.73 = f32[1,1,96,512]{3,2,1,0:T(8,128)} custom-call(f32[1,1,96,512]{3,2,1,0:T(8,128)} %refs_0_.1, f32[1,1,128,7680]{3,2,1,0:T(8,128)} %refs_1_.1, f32[1,1,128,1792]{3,2,1,0:T(8,128)} %refs_2_.1, s32[8,128]{1,0:T(8,128)} %pad.4.refs_3_, s32[1,1,256]{2,1,0:T(1,128)} %refs_4_.1, f32[1,1,512]{2,1,0:T(1,128)} %refs_5_.1, f32[1,1,256]{2,1,0:T(1,128)} %refs_6_.1), custom_call_target="tpu_custom_call" | custom-call | tf_op jit(solution)/shard_map/pallas_call | solution.py:521
  112.6 1.6 %copy.9 = f32[1,1,96,512]{3,2,1,0:T(8,128)} copy(f32[1,1,96,512]{3,2,1,0:T(8,128)} %shard_map.73) | data formatting | bytes 393216

commit v2 on v1

--- a/solution.py
+++ b/solution.py
@@ -12,6 +12,9 @@
 MESH = pl.DeviceIdType.MESH
 F32 = jnp.float32
 BF16 = jnp.bfloat16
+PRE_FROM = 1
+RELAY_FROM = 1
+SHARE = 4
 
 
 def flip(value, mask):
@@ -77,8 +80,11 @@
     def size(self, level):
         return self.fronts << level
 
-    def pre(self, level):
-        return level >= 2
+    def pre(self, key):
+        return self.scatters[key][0] >= (1 if key[0] == "out" else PRE_FROM)
+
+    def relay(self, key):
+        return self.gathers[key][0] >= (1 if key[0] == "rhs" else RELAY_FROM)
 
 
 def kernel(plan, pivots, *refs):
@@ -86,7 +92,7 @@
         rhs_ref,
         inverse_hbm,
         update_hbm,
-        targets_ref,
+        lists_ref,
         pairs_ref,
         diagonal_ref,
         coupling_ref,
@@ -95,6 +101,7 @@
         update_raw,
         inverse_split,
         update_split,
+        targets_ref,
         targets_far,
         targets_smem,
         load_sem,
@@ -122,7 +129,7 @@
     for key in scatter_keys:
         part[key] = buffers.pop(0)
         landed[key] = buffers.pop(0)
-        if plan.pre(plan.scatters[key][0]):
+        if plan.pre(key):
             first[key] = buffers.pop(0)
 
     def rank(level):
@@ -162,19 +169,35 @@
             span, span, send_sem, recv_sem, device_id=peer(0, 1), device_id_type=MESH
         ).wait_send()
 
-    def gather_start(key):
+    bulk = []
+
+    def issue(count):
+        for _ in range(min(count, len(bulk))):
+            bulk.pop(0)()
+
+    def far_first(count):
+        return sorted(range(1, count), key=lambda mask: -bin(mask).count("1"))
+
+    def gather_start(key, later=False):
         level, _ = plan.gathers[key]
         buffer, index = gather_buffer[key], gather_keys.index(key)
         mine = rank(level)
         sems = gather_send.at[index, 0], gather_recv.at[index, 0]
-        for mask in range(1, nx << level):
-            send(buffer.at[mine], buffer.at[mine], *sems, peer(level, mask))
-        sends.append((buffer, (nx << level) - 1, *sems))
+        count = nx << level if plan.relay(key) else fronts << level
+        for mask in far_first(count):
+
+            def one(mask=mask):
+                send(buffer.at[mine], buffer.at[mine], *sems, peer(level, mask))
+
+            bulk.append(one) if later else one()
+        sends.append((buffer, count - 1, *sems))
 
     def gather_forward(key):
         level, _ = plan.gathers[key]
         buffer, index = gather_buffer[key], gather_keys.index(key)
         count = nx << level
+        if not plan.relay(key):
+            return
         wait_recv(buffer, count - 1, gather_send.at[index, 0], gather_recv.at[index, 0])
         span = buffer.at[pl.ds(core * count, count)]
         sems = gather_send.at[index, 1], gather_recv.at[index, 1]
@@ -184,15 +207,17 @@
     def gather_finish(key):
         level, _ = plan.gathers[key]
         index = gather_keys.index(key)
+        step = 1 if plan.relay(key) else 0
+        count = nx << level if step else (fronts << level) - 1
         wait_recv(
-            gather_buffer[key], nx << level, gather_send.at[index, 1], gather_recv.at[index, 1]
+            gather_buffer[key], count, gather_send.at[index, step], gather_recv.at[index, step]
         )
 
     def scatter_start(key):
         level, _ = plan.scatters[key]
         index = scatter_keys.index(key)
         count = nx << level
-        if plan.pre(level):
+        if plan.pre(key):
             sems = scatter_send.at[index, 0], scatter_recv.at[index, 0]
             send(
                 part[key].at[pl.ds((1 - core) * count, count)], first[key], *sems, peer(level, count)
@@ -201,31 +226,38 @@
         else:
             scatter_spread(key, 2 * count)
 
-    def scatter_spread(key, count):
+    def scatter_spread(key, count, later=False):
         level, _ = plan.scatters[key]
         index = scatter_keys.index(key)
         mine = rank(level)
         sems = scatter_send.at[index, 1], scatter_recv.at[index, 1]
-        for mask in range(1, count):
-            send(
-                part[key].at[flip(mine, mask)], landed[key].at[mask - 1], *sems, peer(level, mask)
-            )
+        for mask in far_first(count):
+
+            def one(mask=mask):
+                send(
+                    part[key].at[flip(mine, mask)],
+                    landed[key].at[mask - 1],
+                    *sems,
+                    peer(level, mask),
+                )
+
+            bulk.append(one) if later else one()
         sends.append((part[key], count - 1, *sems))
 
-    def scatter_middle(key):
+    def scatter_middle(key, later=False):
         level, _ = plan.scatters[key]
         index = scatter_keys.index(key)
         count = nx << level
-        if plan.pre(level):
+        if plan.pre(key):
             wait_recv(first[key], count, scatter_send.at[index, 0], scatter_recv.at[index, 0])
             span = pl.ds(core * count, count)
             part[key][span] = part[key][span] + first[key][...]
-            scatter_spread(key, count)
+            scatter_spread(key, count, later)
 
     def scatter_finish(key):
         level, _ = plan.scatters[key]
         index = scatter_keys.index(key)
-        count = (nx << level) if plan.pre(level) else fronts << level
+        count = (nx << level) if plan.pre(key) else fronts << level
         wait_recv(landed[key], count - 1, scatter_send.at[index, 1], scatter_recv.at[index, 1])
         total = part[key][rank(level)]
         for place in range(count - 1):
@@ -256,6 +288,9 @@
         gather_buffer["rhs", level][rank(level)] = rhs_ref[
             0, 0, :, level * pivots : (level + 1) * pivots
         ]
+
+    targets_ref[...] = jnp.zeros_like(targets_ref)
+    targets_ref[:1, : lists_ref.shape[1]] = lists_ref[...]
 
     barrier = pltpu.get_barrier_semaphore()
     everyone = plan.size(LEVELS - 1)
@@ -287,29 +322,18 @@
         blocks = range(start // BLOCK, stop // BLOCK)
         return jnp.concatenate([inverse_split[block] for block in blocks], 1)
 
+    def prepare_update(level):
+        cols = slice(update_start(level), update_start(level + 1))
+        high, low = split(update_raw[:, cols])
+        update_split[:pivots, cols] = high
+        update_split[pivots:, cols] = low
+
+    for level in range(2, LEVELS):
+        gather_start(("rhs", level), later=True)
+    issue(SHARE)
     prepare(0)
     loads[LEVELS].wait()
-    high, low = split(update_raw[...])
-    update_split[:pivots] = high
-    update_split[pivots:] = low
-
-    count = diagonal_ref.shape[2]
-    from_pair = (
-        lax.div(lax.broadcasted_iota(jnp.int32, (count // 2, count), 1), 2)
-        == lax.broadcasted_iota(jnp.int32, (count // 2, count), 0)
-    ).astype(F32)
-    pair_rows = jnp.concatenate(
-        [
-            jnp.broadcast_to(coupling_ref[0], (8, count // 2)),
-            jnp.broadcast_to(pairs_ref[0].astype(F32), (8, count // 2)),
-        ],
-        0,
-    )
-    repeated = jnp.dot(
-        pair_rows, from_pair, precision=lax.Precision.HIGHEST, preferred_element_type=F32
-    )
-    couple, flags = repeated[:8], repeated[8:] > 0.5
-    diagonal = jnp.broadcast_to(diagonal_ref[0], (8, count))
+    prepare_update(0)
 
     def swap(values):
         width = values.shape[1]
@@ -318,28 +342,54 @@
             even, pltpu.roll(values, width - 1, 1), pltpu.roll(values, 1, 1)
         )
 
-    other_diagonal = swap(diagonal)
-    determinant = diagonal * other_diagonal - couple * couple
-    straight = jnp.where(flags, other_diagonal / determinant, 1.0 / diagonal)[:1]
-    crossed = jnp.where(flags, -couple / determinant, 0.0)[:1]
-
-    def pivot_solve(solved, level):
+    def pivot_coefficients():
+        width = diagonal_ref.shape[2]
+        from_pair = (
+            lax.div(lax.broadcasted_iota(jnp.int32, (width // 2, width), 1), 2)
+            == lax.broadcasted_iota(jnp.int32, (width // 2, width), 0)
+        ).astype(F32)
+        pair_rows = jnp.concatenate(
+            [
+                jnp.broadcast_to(coupling_ref[0], (8, width // 2)),
+                jnp.broadcast_to(pairs_ref[0].astype(F32), (8, width // 2)),
+            ],
+            0,
+        )
+        repeated = jnp.dot(
+            pair_rows, from_pair, precision=lax.Precision.HIGHEST, preferred_element_type=F32
+        )
+        couple, flags = repeated[:8], repeated[8:] > 0.5
+        diagonal = jnp.broadcast_to(diagonal_ref[0], (8, width))
+
+        other_diagonal = swap(diagonal)
+        determinant = diagonal * other_diagonal - couple * couple
+        straight = jnp.where(flags, other_diagonal / determinant, 1.0 / diagonal)[:1]
+        crossed = jnp.where(flags, -couple / determinant, 0.0)[:1]
+        return straight, crossed
+
+    def pivot_solve(solved, level, straight, crossed):
         span = slice(level * pivots, (level + 1) * pivots)
         return solved * straight[:, span] + swap(solved) * crossed[:, span]
 
-    for level in range(LEVELS - 1):
-        pltpu.make_async_remote_copy(
-            targets_ref,
-            targets_far.at[level],
-            targets_send.at[level],
-            targets_recv.at[level],
-            device_id=(flip(leaf, 1 << level), front),
-            device_id_type=MESH,
-        ).wait()
-    lists = [targets_ref] + [targets_far.at[level] for level in range(LEVELS - 1)]
-    for index, source in enumerate(lists):
-        pltpu.make_async_copy(source, targets_smem.at[index], load_sem.at[LEVELS + 1]).start()
-        pltpu.make_async_copy(source, targets_smem.at[index], load_sem.at[LEVELS + 1]).wait()
+    def fetch_lists():
+        for level in range(LEVELS - 1):
+            pltpu.make_async_remote_copy(
+                targets_ref,
+                targets_far.at[level],
+                targets_send.at[level],
+                targets_recv.at[level],
+                device_id=(flip(leaf, 1 << level), front),
+                device_id_type=MESH,
+            ).wait()
+        lists = [targets_ref] + [targets_far.at[level] for level in range(LEVELS - 1)]
+        copies = [
+            pltpu.make_async_copy(source, targets_smem.at[index], load_sem.at[LEVELS + 1 + index])
+            for index, source in enumerate(lists)
+        ]
+        for copy in copies:
+            copy.start()
+        for copy in copies:
+            copy.wait()
 
     def block_count(level):
         return 2 * pivots * (1 << level) // BLOCK
@@ -381,7 +431,6 @@
         return halves
 
     weighted = []
-    gather_forward(("rhs", 0))
     gather_finish(("rhs", 0))
     product = known_part(0)
     for level in range(LEVELS):
@@ -403,7 +452,6 @@
                         rows_of(jnp.concatenate(values, 1)), jnp.concatenate(matrices, 1)
                     )
         solved = fold(product, sides, pivots)
-        weighted.append(pivot_solve(solved, level))
         if level + 1 < LEVELS:
             key = ("up", level)
             start = update_start(level)
@@ -417,20 +465,31 @@
                         i * half : (i + 1) * half, index * BLOCK : (index + 1) * BLOCK
                     ]
             scatter_start(key)
+            issue(SHARE)
+            if level == 0:
+                coefficients = pivot_coefficients()
+            weighted.append(pivot_solve(solved, level, *coefficients))
+            scatter_middle(key)
+            if plan.pre(key):
+                issue(SHARE)
             prepare(level + 1)
-            scatter_middle(key)
+            if level + 2 < LEVELS:
+                prepare_update(level + 1)
             if level == 0:
-                gather_forward(("rhs", 1))
+                fetch_lists()
+            if level + 2 == LEVELS:
+                issue(len(bulk))
+            gather_forward(("rhs", level + 1))
             total = scatter_finish(key)
             gather_buffer[key][rank(level + 1)] = total
             gather_start(key)
-            if level + 2 < LEVELS:
-                gather_start(("rhs", level + 2))
-            if level:
-                gather_forward(("rhs", level + 1))
+            issue(SHARE)
             gather_finish(("rhs", level + 1))
             product = known_part(level + 1)
             gather_forward(key)
+            issue(SHARE)
+        else:
+            weighted.append(pivot_solve(solved, level, *coefficients))
 
     for level in reversed(range(LEVELS)):
         target = weighted[level]
@@ -467,6 +526,8 @@
                                 i * half : (i + 1) * half, j * BLOCK : (j + 1) * BLOCK
                             ]
             scatter_start(key)
+            scatter_middle(key)
+            issue(SHARE)
         out_key = ("out", level)
         step = 2 if level else 1
         for slot in range(0, plan.size(level), step):
@@ -474,17 +535,16 @@
             partial = across(square, inverse_columns(start, start + step * pivots), sides)
             for i in range(step):
                 part[out_key][slot + i] = partial[:, i * pivots : (i + 1) * pivots]
+        scatter_start(out_key)
         if level:
-            scatter_middle(key)
             total = scatter_finish(key)
             gather_buffer[key][rank(level - 1)] = total
             gather_start(key)
-            scatter_start(out_key)
+            scatter_middle(out_key, later=True)
+            issue(SHARE)
             gather_forward(key)
-            scatter_middle(out_key)
-        else:
-            scatter_start(out_key)
-            scatter_middle(out_key)
+            issue(SHARE)
+    issue(len(bulk))
     for level in reversed(range(LEVELS)):
         out_ref[0, 0, :, level * pivots : (level + 1) * pivots] = scatter_finish(("out", level))
     for item in sends:
@@ -506,14 +566,14 @@
     fronts = lax.axis_size("front")
     plan = Plan(fronts, sides)
     nx = fronts // 2
-    targets = jnp.pad(update_targets, ((0, 7), (0, BLOCK - update_targets.shape[1])))
+    targets = jax.ShapeDtypeStruct((8, BLOCK), jnp.int32)
     buffers = []
     for level, rows in plan.gathers.values():
         buffers.append(pltpu.VMEM((plan.size(level), rows, pivots), F32))
-    for level, rows in plan.scatters.values():
+    for key, (level, rows) in plan.scatters.items():
         buffers.append(pltpu.VMEM((plan.size(level), rows, pivots), F32))
         buffers.append(pltpu.VMEM((plan.size(level), rows, pivots), F32))
-        if plan.pre(level):
+        if plan.pre(key):
             buffers.append(pltpu.VMEM((nx << level, rows, pivots), F32))
     vmem = pl.BlockSpec(memory_space=pltpu.VMEM)
     hbm = pl.BlockSpec(memory_space=pl.ANY)
@@ -528,9 +588,10 @@
             pltpu.VMEM(update_panel.shape[2:], F32),
             pltpu.VMEM((factor_inverse.shape[3] // BLOCK, 2 * pivots, BLOCK), BF16),
             pltpu.VMEM((2 * pivots, update_panel.shape[3]), BF16),
+            pltpu.VMEM(targets.shape, jnp.int32),
             pltpu.VMEM((LEVELS - 1,) + targets.shape, jnp.int32),
             pltpu.SMEM((LEVELS,) + targets.shape, jnp.int32),
-            dma((LEVELS + 2,)),
+            dma((2 * LEVELS + 1,)),
             dma((LEVELS - 1,)),
             dma((LEVELS - 1,)),
             dma((len(plan.gathers), 2)),
@@ -544,7 +605,7 @@
         right_side,
         factor_inverse,
         update_panel,
-        targets,
+        update_targets,
         pivot_pairs,
         pivot_diagonal,
         pivot_coupling,

time: 116 us -> 103 us (0.89); the launches traced: 114 us -> 102 us
  Pallas kernels: 111 us -> 101 us
  local copies, waits for them, and re-layouts: 2.87 us -> 1.62 us
    pallas_call x1, Pallas kernels: 111 us -> 101 us  [per_device(): pl.pallas_call(functools.partial(kernel, plan, pivots), out_shape=jax.Sha...]
    pad x1 -> x0, local copies, waits for them, and re-layouts: 1.25 us -> none  [per_device(): jnp.pad(update_targets, ((0, 7), (0, BLOCK - update_targets.shape[1])))]
where the time goes in v2:
time: 103 us; the launch traced here: 102 us
  Pallas kernels  101 us (98%)
  local copies, waits for them, and re-layouts  1.62 us (2%)
    pallas_call x1, Pallas kernels, per_device(): pl.pallas_call(functools.partial(kernel, plan, pivots), out_shape=jax.Sha...  101 us

profile of v2, /device:TPU:0, one launch (start us, length us, event | category | flops | bytes accessed | tf_op | source)
XLA Modules:
  0.0 102.5 jit_solution(785204202912397555)
XLA Ops:
  0.0 100.9 %shard_map.73 = f32[1,1,96,512]{3,2,1,0:T(8,128)} custom-call(f32[1,1,96,512]{3,2,1,0:T(8,128)} %refs_0_.1, f32[1,1,128,7680]{3,2,1,0:T(8,128)} %refs_1_.1, f32[1,1,128,1792]{3,2,1,0:T(8,128)} %refs_2_.1, s32[1,14]{1,0:T(1,128)} %refs_3_.1, s32[1,1,256]{2,1,0:T(1,128)} %refs_4_.1, f32[1,1,512]{2,1,0:T(1,128)} %refs_5_.1, f32[1,1,256]{2,1,0:T(1,128)} %refs_6_.1), custom_call_target="tpu_custom_call" | custom-call | tf_op jit(solution)/shard_map/pallas_call | solution.py:581
  100.9 1.6 %copy.9 = f32[1,1,96,512]{3,2,1,0:T(8,128)} copy(f32[1,1,96,512]{3,2,1,0:T(8,128)} %shard_map.73) | data formatting | bytes 393216
